TPU v7x, 32 devices: a whole 2x2x4 slice. The times are simulated.
32 devices in a mesh: batch: 4 (over y, core), tensor: 2 (over x), latent: 4 (over z).
Axes of the slice: x: 2, y: 2, z: 4, core: 2. Of those that a mesh axis runs over, the one named last changes fastest.
Arguments:
- residual: bfloat16 [1024, 3584], P('batch', ('tensor', 'latent')), may hold values from -6 to 6
- target: bfloat16 [1024, 3584], P('batch', ('tensor', 'latent')), may hold values from -6 to 6
- encoder_weight: bfloat16 [3584, 32768], P(None, ('tensor', 'latent')), may hold values from -0.09375 to 0.09375
- encoder_bias: bfloat16 [32768], P(('tensor', 'latent')), may hold values from -0.59765625 to 0.29882812
- decoder_weight: bfloat16 [32768, 3584], P(('tensor', 'latent')), may hold values from -0.0625 to 0.0625
- decoder_bias: bfloat16 [3584], replicated, may hold values from -3 to 3
- first_gain: bfloat16 [3584], replicated, may hold values from 0.5 to 1.5
- second_gain: bfloat16 [3584], replicated, may hold values from 0.5 to 1.5
- gate_weight: bfloat16 [3584, 7168], P(None, ('tensor', 'latent')), may hold values from -0.09375 to 0.09375
- up_weight: bfloat16 [3584, 7168], P(None, ('tensor', 'latent')), may hold values from -0.09375 to 0.09375
- down_weight: bfloat16 [7168, 3584], P(('tensor', 'latent')), may hold values from -0.09375 to 0.09375
Outputs:
- encoder_grad: bfloat16 [3584, 32768], P('batch', ('tensor', 'latent'))
- decoder_grad: bfloat16 [32768, 3584], P(('tensor', 'latent'), 'batch')
All inputs are finite; a program needn't handle non-finite values.
Results may differ from a plain program's by a relative error of at most 0.012.
The roundings to bfloat16 on the way count: a program that leaves them out, or rounds other values in their place, can miss the bound.
Values may be sent and summed in bfloat16 or wider, within the bound.
A program may use at most 192 MiB of HBM per device.

v0:
```python
import jax
import jax.numpy as jnp
from jax import lax
from jax.sharding import PartitionSpec as P

epsilon = 1e-06


def per_device(
    residual,
    target,
    encoder_weight,
    encoder_bias,
    decoder_weight,
    decoder_bias,
    first_gain,
    second_gain,
    gate_weight,
    up_weight,
    down_weight,
):
    f32 = jnp.float32
    bf16 = jnp.bfloat16
    contract_last = (((1,), (1,)), ((), ()))
    contract_first = (((0,), (0,)), ((), ()))
    share_width = residual.shape[1]
    model_width = share_width * lax.axis_size(("tensor", "latent"))
    offset = lax.axis_index(("tensor", "latent")) * share_width
    token_count = residual.shape[0] * lax.axis_size("batch")
    bias_share = lax.dynamic_slice_in_dim(decoder_bias.astype(f32), offset, share_width)
    first_share = lax.dynamic_slice_in_dim(first_gain.astype(f32), offset, share_width)
    second_share = lax.dynamic_slice_in_dim(second_gain.astype(f32), offset, share_width)
    centered_share = (residual.astype(f32) - bias_share).astype(bf16)
    centered = lax.all_gather(centered_share, ("tensor", "latent"), axis=1, tiled=True)
    preact = jnp.dot(centered, encoder_weight, preferred_element_type=f32) + encoder_bias.astype(
        f32
    )
    latents = jnp.maximum(preact, 0.0).astype(bf16)
    partial_recon = jnp.dot(latents, decoder_weight, preferred_element_type=f32)
    recon_full = lax.psum(partial_recon.astype(jnp.bfloat16), ("tensor", "latent")).astype(
        jnp.float32
    ) + decoder_bias.astype(f32)
    scale_in = lax.rsqrt(
        jnp.sum(recon_full * recon_full, axis=1, keepdims=True) / model_width + epsilon
    )
    normed_input = (recon_full * scale_in * first_gain.astype(f32)).astype(bf16)
    recon = lax.dynamic_slice_in_dim(recon_full, offset, share_width, 1)
    gate_value = jnp.dot(normed_input, gate_weight, preferred_element_type=f32)
    up_value = jnp.dot(normed_input, up_weight, preferred_element_type=f32)
    gelu_value, gelu_back = jax.vjp(lambda v: jax.nn.gelu(v, approximate=True), gate_value)
    hidden = (gelu_value * up_value).astype(bf16)
    partial_out = jnp.dot(hidden, down_weight, preferred_element_type=f32)
    output = lax.psum_scatter(
        partial_out.astype(jnp.bfloat16), ("tensor", "latent"), scatter_dimension=1, tiled=True
    ).astype(jnp.float32)
    out_squares = lax.psum(jnp.sum(output * output, axis=1), ("tensor", "latent"))
    scale_out = lax.rsqrt(out_squares[:, None] / model_width + epsilon)
    normed_out = output * scale_out
    result = recon + normed_out * second_share
    grad_result = 2.0 * (result - target.astype(f32)) / token_count
    grad_normed = grad_result * second_share
    inner_out = (
        lax.psum(jnp.sum(grad_normed * normed_out, axis=1), ("tensor", "latent")) / model_width
    )
    grad_share = (scale_out * (grad_normed - normed_out * inner_out[:, None])).astype(bf16)
    grad_output = lax.all_gather(grad_share, ("tensor", "latent"), axis=1, tiled=True)
    grad_hidden = lax.dot_general(
        grad_output, down_weight, contract_last, preferred_element_type=f32
    )
    grad_gate = gelu_back(grad_hidden * up_value)[0].astype(bf16)
    grad_up = (grad_hidden * gelu_value).astype(bf16)
    partial_input = lax.dot_general(
        grad_gate, gate_weight, contract_last, preferred_element_type=f32
    )
    partial_input = partial_input + lax.dot_general(
        grad_up, up_weight, contract_last, preferred_element_type=f32
    )
    grad_normed_in = lax.psum_scatter(
        partial_input.astype(jnp.bfloat16), ("tensor", "latent"), scatter_dimension=1, tiled=True
    ).astype(jnp.float32)
    unit = recon * scale_in
    grad_unit = grad_normed_in * first_share
    inner_in = lax.psum(jnp.sum(grad_unit * unit, axis=1), ("tensor", "latent")) / model_width
    recon_share = (grad_result + scale_in * (grad_unit - unit * inner_in[:, None])).astype(bf16)
    grad_recon = lax.all_gather(recon_share, ("tensor", "latent"), axis=1, tiled=True)
    grad_latent = lax.dot_general(
        grad_recon, decoder_weight, contract_last, preferred_element_type=f32
    )
    grad_preact = jnp.where(preact > 0, grad_latent, 0.0).astype(bf16)
    centered_block, recon_block = (
        lax.all_to_all(centered, "batch", split_axis=1, concat_axis=0, tiled=True),
        lax.all_to_all(grad_recon, "batch", split_axis=1, concat_axis=0, tiled=True),
    )
    latents_all, preact_all = (
        lax.all_gather(latents, "batch", axis=0, tiled=True),
        lax.all_gather(grad_preact, "batch", axis=0, tiled=True),
    )
    encoder_grad = lax.dot_general(
        centered_block, preact_all, contract_first, preferred_element_type=f32
    )
    decoder_grad = lax.dot_general(
        latents_all, recon_block, contract_first, preferred_element_type=f32
    )
    return (encoder_grad.astype(bf16), decoder_grad.astype(bf16))


def solution(mesh):
    in_specs = (
        P("batch", ("tensor", "latent")),
        P("batch", ("tensor", "latent")),
        P(None, ("tensor", "latent")),
        P(("tensor", "latent")),
        P(("tensor", "latent"), None),
        P(),
        P(),
        P(),
        P(None, ("tensor", "latent")),
        P(None, ("tensor", "latent")),
        P(("tensor", "latent"), None),
    )
    out_specs = (P("batch", ("tensor", "latent")), P(("tensor", "latent"), "batch"))
    return jax.shard_map(
        per_device, mesh=mesh, in_specs=in_specs, out_specs=out_specs, check_vma=False
    )
```

profile of v0, /device:TPU:0, one launch (start us, length us, event | category | flops | bytes accessed | tf_op | source)
XLA Modules:
  0.0 670.3 jit_solution(1007464066563289429)
XLA Ops:
  10.5 49.3 %all-gather.6.cloned.1.call-done = bf16[256,3584]{0,1:T(8,128)(2,1)} async-done(((bf16[256,448]{0,1:T(8,128)(2,1)}), bf16[256,3584]{0,1:T(8,128)(2,1)}) %all-gather.6.cloned.1.call-update) | async-done | bytes 1835024 | tf_op jit(solution)/shard_map/all_gather | solution.py:34
  59.8 15.2 %maximum_convert_fusion = (bf16[256,4096]{1,0:T(8,128)(2,1)S(1)}, f32[256,4096]{1,0:T(8,128)}) fusion(f32[4096]{0:T(1024)S(1)} %convert_element_type.74, bf16[256,3584]{0,1:T(8,128)(2,1)} %all-gather.6.cloned.1.call-done, bf16[3584,4096]{1,0:T(8,128)(2,1)} %param.13), kind=kOutput, calls=%fused_computation.11 | convolution fusion | flops 7519338496 | bytes 37502976 | tf_op jit(solution)/shard_map/dot_general | solution.py:35
  75.0 15.5 %convolution_convert_fusion.2 = bf16[256,3584]{1,0:T(8,128)(2,1)} fusion(bf16[256,4096]{1,0:T(8,128)(2,1)S(1)} %get-tuple-element.4, bf16[4096,3584]{1,0:T(8,128)(2,1)} %param.15), kind=kOutput, calls=%fused_computation.5 | convolution fusion | flops 7517110272 | bytes 33292288 | tf_op jit(solution)/shard_map/dot_general | solution.py:39
  90.7 94.5 %all-reduce.2.cloned.1.call-done = bf16[256,3584]{1,0:T(8,128)(2,1)} async-done(((bf16[256,3584]{1,0:T(8,128)(2,1)}), bf16[256,3584]{1,0:T(8,128)(2,1)}) %all-reduce.2.cloned.1.call-update) | async-done | bytes 1835024 | tf_op jit(solution)/shard_map/psum | solution.py:40
  185.2 4.0 convert_add_fusion
  189.2 5.6 fusion.30
  197.1 4.3 fusion.2
  203.1 64.5 %reduce-scatter.7.cloned.1.call-done = bf16[448,256]{1,0:T(8,128)(2,1)} async-done(((bf16[3584,256]{1,0:T(8,128)(2,1)}), bf16[448,256]{1,0:T(8,128)(2,1)}) %reduce-scatter.7.cloned.1.call-update) | async-done | bytes 229392
  268.9 19.4 %psum.29 = f32[256]{0:T(256)S(1)} all-reduce(f32[256]{0:T(256)S(1)} %fusion.20), channel_id=1, replica_groups=mesh['batch'=4,'tensor'=2,'latent'=4] {'tensor','latent'}, use_global_device_ids=true, to_apply=%region_4.0 | all-reduce | flops 256 | bytes 2048 | tf_op jit(solution)/shard_map/psum | solution.py:56
  289.7 17.2 %psum.30 = f32[256]{0:T(256)S(1)} all-reduce(f32[256]{0:T(256)S(1)} %fusion.16), channel_id=1, replica_groups=mesh['batch'=4,'tensor'=2,'latent'=4] {'tensor','latent'}, use_global_device_ids=true, to_apply=%region_6.0 | all-reduce | flops 256 | bytes 2048 | tf_op jit(solution)/shard_map/psum | solution.py:63
  309.5 45.8 %all-gather.8.cloned.1.call-done = bf16[256,3584]{0,1:T(8,128)(2,1)} async-done(((bf16[256,448]{0,1:T(8,128)(2,1)}), bf16[256,3584]{0,1:T(8,128)(2,1)}) %all-gather.8.cloned.1.call-update) | async-done | bytes 1835024 | tf_op jit(solution)/shard_map/all_gather | solution.py:66
  355.3 5.6 fusion.45
  361.0 5.4 fusion.21
  366.5 3.6 fusion.3
  370.3 65.2 %reduce-scatter.9.cloned.1.call-done = bf16[448,256]{1,0:T(8,128)(2,1)} async-done(((bf16[3584,256]{1,0:T(8,128)(2,1)}), bf16[448,256]{1,0:T(8,128)(2,1)}) %reduce-scatter.9.cloned.1.call-update) | async-done | bytes 229392
  438.0 19.3 %psum.31 = f32[256]{0:T(256)S(1)} all-reduce(f32[256]{0:T(256)S(1)} %multiply_reduce_fusion.1), channel_id=1, replica_groups=mesh['batch'=4,'tensor'=2,'latent'=4] {'tensor','latent'}, use_global_device_ids=true, to_apply=%region_9.0 | all-reduce | flops 256 | bytes 2048 | tf_op jit(solution)/shard_map/psum | solution.py:83
  460.5 44.0 %all-gather.10.cloned.1.call-done = bf16[256,3584]{0,1:T(8,128)(2,1)} async-done(((bf16[256,448]{0,1:T(8,128)(2,1)}), bf16[256,3584]{0,1:T(8,128)(2,1)}) %all-gather.10.cloned.1.call-update) | async-done | bytes 1835024 | tf_op jit(solution)/shard_map/all_gather | solution.py:85
  504.5 18.3 %fusion = bf16[256,4096]{1,0:T(8,128)(2,1)} fusion(bf16[256,3584]{0,1:T(8,128)(2,1)} %all-gather.10.cloned.1.call-done, bf16[4096,3584]{1,0:T(8,128)(2,1)} %param.15, f32[256,4096]{1,0:T(8,128)} %get-tuple-element.5), kind=kOutput, calls=%fused_computation.6 | convolution fusion | flops 7519338496 | bytes 37486592 | tf_op jit(solution)/shard_map/dot_general | solution.py:86
  522.8 46.2 %all_to_all.38 = bf16[256,4,896]{0,2,1:T(8,128)(2,1)} all-to-all(bf16[256,4,896]{0,2,1:T(8,128)(2,1)S(1)} %bitcast.35), channel_id=1, replica_groups=mesh['batch'=4,'tensor'=2,'latent'=4] {'batch'}, dimensions={1} | all-to-all | bytes 3670016 | tf_op jit(solution)/shard_map/all_to_all | solution.py:91
  569.0 3.8 all-to-all-start.1
  576.5 24.1 %all-to-all-done.1 = bf16[256,4,896]{0,2,1:T(8,128)(2,1)S(1)} async-done(((bf16[256,4,896]{0,2,1:T(8,128)(2,1)}), bf16[256,4,896]{0,2,1:T(8,128)(2,1)S(1)}, u32[]{:S(2)}, u32[]{:S(2)}) %all-to-all-start.1) | async-done | bytes 1835040 | tf_op jit(solution)/shard_map/all_to_all | solution.py:92
  603.0 15.2 %convolution_convert_fusion = bf16[4096,896]{1,0:T(8,128)(2,1)} fusion(bf16[1024,4096]{1,0:T(8,128)(2,1)} %all-gather.14.cloned.1.call-done, bf16[1024,896]{1,0:T(8,128)(2,1)} %bitcast.38), kind=kOutput, calls=%fused_computation | convolution fusion | flops 7519862784 | bytes 17563648 | tf_op jit(solution)/shard_map/dot_general | solution.py:101
  618.1 33.3 %all-gather.12.cloned.1.call-done = bf16[1024,4096]{1,0:T(8,128)(2,1)} async-done(((bf16[256,4096]{1,0:T(8,128)(2,1)}), bf16[1024,4096]{1,0:T(8,128)(2,1)}) %all-gather.12.cloned.1.call-update) | async-done | bytes 8388624 | tf_op jit(solution)/shard_map/all_gather | solution.py:96
  651.4 12.1 %convolution_convert_fusion.1 = bf16[896,4096]{1,0:T(8,128)(2,1)} fusion(bf16[1024,896]{1,0:T(8,128)(2,1)S(1)} %bitcast.37, bf16[1024,4096]{1,0:T(8,128)(2,1)} %all-gather.12.cloned.1.call-done), kind=kOutput, calls=%fused_computation.1 | convolution fusion | flops 7519862784 | bytes 17563648 | tf_op jit(solution)/shard_map/dot_general | solution.py:98
  (71 shorter events, 24.4 us)
Async XLA Ops:
  7.2 52.6 %all-gather.6.cloned.1.call-start = ((), (), s32[]{:S(2)}) async-start(), calls=%async_computation.4 | async-start | bytes 2064384 | tf_op jit(solution)/shard_map/all_gather | solution.py:34
  9.8 175.5 %all-reduce.2.cloned.1.call-start = ((), (), s32[]{:S(2)}) async-start(), calls=%async_computation.5 | async-start | bytes 3670016 | tf_op jit(solution)/shard_map/psum | solution.py:40
  75.0 15.5 %copy-start = (bf16[256,4096]{1,0:T(8,128)(2,1)}, bf16[256,4096]{1,0:T(8,128)(2,1)S(1)}, u32[]{:S(2)}) copy-start(bf16[256,4096]{1,0:T(8,128)(2,1)S(1)} %get-tuple-element.4) | copy-start | bytes 6291460
  75.0 15.8 %copy-start.5 = (bf16[3584]{0:T(1024)(128)(2,1)S(1)}, bf16[3584]{0:T(1024)(128)(2,1)}, u32[]{:S(2)}) copy-start(bf16[3584]{0:T(1024)(128)(2,1)} %param.16) | copy-start | bytes 21508
  75.0 15.8 %copy-start.6 = (bf16[3584]{0:T(1024)(128)(2,1)S(1)}, bf16[3584]{0:T(1024)(128)(2,1)}, u32[]{:S(2)}) copy-start(bf16[3584]{0:T(1024)(128)(2,1)} %param.17) | copy-start | bytes 21508
  90.5 177.2 %reduce-scatter.7.cloned.1.call-start = ((), (), s32[]{:S(2)}) async-start(), calls=%async_computation.10 | async-start | bytes 2064384
  185.2 9.6 %slice-start = ((s8[6422528]{0:T(1024)(128)(4,1)}), s8[4194304]{0:T(1024)(128)(4,1)S(1)}, s32[]{:S(2)}) async-start(s8[6422528]{0:T(1024)(128)(4,1)} %bitcast.29), calls=%async_computation.12 | async-start | bytes 8388608
  189.2 5.7 slice-start.1
  189.2 5.7 copy-start.3
  189.2 7.9 %slice-start.4 = ((s8[6422528]{0:T(1024)(128)(4,1)}), s8[4194304]{0:T(1024)(128)(4,1)S(1)}, s32[]{:S(2)}) async-start(s8[6422528]{0:T(1024)(128)(4,1)} %bitcast.41), calls=%async_computation.16 | async-start | bytes 8388608
  194.9 2.2 slice-start.5
  197.1 4.4 copy-start.4
  201.4 154.0 %all-gather.8.cloned.1.call-start = ((), (), s32[]{:S(2)}) async-start(), calls=%async_computation.6 | async-start | bytes 2064384 | tf_op jit(solution)/shard_map/all_gather | solution.py:66
  309.2 126.3 %reduce-scatter.9.cloned.1.call-start = ((), (), s32[]{:S(2)}) async-start(), calls=%async_computation.11 | async-start | bytes 2064384
  355.3 11.1 %slice-start.2 = ((s8[6422528]{0:T(1024)(128)(4,1)}), s8[2228224]{0:T(1024)(128)(4,1)S(1)}, s32[]{:S(2)}) async-start(s8[6422528]{0:T(1024)(128)(4,1)} %bitcast.31), calls=%async_computation.14 | async-start | bytes 4456448
  361.0 5.5 slice-start.3
  370.1 134.3 %all-gather.10.cloned.1.call-start = ((), (), s32[]{:S(2)}) async-start(), calls=%async_computation.7 | async-start | bytes 2064384 | tf_op jit(solution)/shard_map/all_gather | solution.py:85
  459.7 143.3 %all-gather.14.cloned.1.call-start = ((), (), s32[]{:S(2)}) async-start(), calls=%async_computation.9 | async-start | bytes 10485760 | tf_op jit(solution)/shard_map/all_gather | solution.py:95
  460.4 191.0 %all-gather.12.cloned.1.call-start = ((), (), s32[]{:S(2)}) async-start(), calls=%async_computation.8 | async-start | bytes 10485760 | tf_op jit(solution)/shard_map/all_gather | solution.py:96
  504.5 18.4 %copy-start.1 = (bf16[256,3584]{0,1:T(8,128)(2,1)S(1)}, bf16[256,3584]{0,1:T(8,128)(2,1)}, u32[]{:S(2)}) copy-start(bf16[256,3584]{0,1:T(8,128)(2,1)} %all-gather.6.cloned.1.call-done) | copy-start | bytes 5505028
  569.0 31.6 %all-to-all-start.1 = ((bf16[256,4,896]{0,2,1:T(8,128)(2,1)}), bf16[256,4,896]{0,2,1:T(8,128)(2,1)S(1)}, u32[]{:S(2)}, u32[]{:S(2)}) async-start(bf16[256,4,896]{0,2,1:T(8,128)(2,1)} %bitcast.36), calls=%async_computation.1 | async-start | bytes 3670016 | tf_op jit(solution)/shard_map/all_to_all | solution.py:92
  603.0 48.5 %copy-start.2 = (bf16[4,256,896]{2,1,0:T(8,128)(2,1)S(1)}, bf16[4,256,896]{2,1,0:T(8,128)(2,1)}, u32[]{:S(2)}) copy-start(bf16[4,256,896]{2,1,0:T(8,128)(2,1)} %copy.34) | copy-start | bytes 5505028
Sparse Core Ops, SparseCore 0:
  10.6 49.1 all-gather.5
  90.6 94.5 all-reduce.1
  201.5 66.1 reduce-scatter.6
  309.4 45.9 all-gather.7
  370.3 65.1 reduce-scatter.8
  459.8 44.6 all-gather.9
  506.0 81.8 all-gather.13
  590.1 61.2 all-gather.11
where the time goes:
time: 671 us; the launch traced here: 670 us
  waiting for transfers between devices  422 us (63%)
  matrix products  103 us (15%)
  blocking collectives  102 us (15%)
  between operations  14.4 us (2%)
  other arithmetic  13.9 us (2%)
  local copies, waits for them, and re-layouts  10.9 us (2%)
    unnamed x10, waiting for transfers between devices  131 us
    psum x1, waiting for transfers between devices, per_device(): lax.psum(partial_recon.astype(jnp.bfloat16), ('tensor', 'latent'))  94.5 us
    all_gather x1, waiting for transfers between devices, per_device(): lax.all_gather(centered_share, ('tensor', 'latent'), axis=1, tiled=True)  49.3 us
    all_to_all x1, blocking collectives, per_device(): lax.all_to_all(centered, 'batch', split_axis=1, concat_axis=0, tiled=True)  46.2 us
    all_gather x1, waiting for transfers between devices, per_device(): lax.all_gather(grad_share, ('tensor', 'latent'), axis=1, tiled=True)  45.8 us
    all_gather x1, waiting for transfers between devices, per_device(): lax.all_gather(recon_share, ('tensor', 'latent'), axis=1, tiled=True)  44 us
    all_gather x1, waiting for transfers between devices, per_device(): lax.all_gather(grad_preact, 'batch', axis=0, tiled=True)  33.3 us
    all_to_all x1, waiting for transfers between devices, per_device(): lax.all_to_all(grad_recon, 'batch', split_axis=1, concat_axis=0, tiled=True)  24.1 us
  transfers between devices with their start and end apart: 9, of which 8 were waited for; matrix products, arithmetic and copies ran while one was open for 6% of the time, Pallas kernels for 0%

commit v1 on v0

--- a/solution.py
+++ b/solution.py
@@ -37,7 +37,7 @@
     )
     latents = jnp.maximum(preact, 0.0).astype(bf16)
     partial_recon = jnp.dot(latents, decoder_weight, preferred_element_type=f32)
-    recon_full = lax.psum(partial_recon.astype(jnp.bfloat16), ("tensor", "latent")).astype(
+    recon_full = lax.psum(lax.psum(partial_recon.astype(jnp.bfloat16), "latent"), "tensor").astype(
         jnp.float32
     ) + decoder_bias.astype(f32)
     scale_in = lax.rsqrt(

time: 671 us -> 712 us (1.061)
  waiting for transfers between devices: 422 us -> 462 us
    psum x1 -> x2, waiting for transfers between devices: 94.5 us -> 135 us  [the longest x1 76.4 us: per_device(): lax.psum(partial_recon.astype(jnp.bfloat16), 'latent')]
    unnamed x10 -> x11, waiting for transfers between devices: 131 us -> 131 us
  transfers between devices with their start and end apart: 9 -> 10, of which waited for: 8 -> 9; matrix products, arithmetic and copies ran while one was open for 6% -> 6% of each run, Pallas kernels for 0% -> 0%
where the time goes in v1:
time: 712 us; the launch traced here: 711 us
  waiting for transfers between devices  462 us (65%)
  matrix products  103 us (14%)
  blocking collectives  102 us (14%)
  between operations  14.1 us (2%)
  other arithmetic  13.9 us (2%)
  local copies, waits for them, and re-layouts  10.9 us (2%)
    unnamed x11, waiting for transfers between devices  131 us
    psum x1, waiting for transfers between devices, per_device(): lax.psum(partial_recon.astype(jnp.bfloat16), 'latent')  76.4 us
    psum x1, waiting for transfers between devices, per_device(): lax.psum(lax.psum(partial_recon.astype(jnp.bfloat16), 'latent'), 'tensor')  58.3 us
    all_gather x1, waiting for transfers between devices, per_device(): lax.all_gather(centered_share, ('tensor', 'latent'), axis=1, tiled=True)  49.3 us
    all_to_all x1, blocking collectives, per_device(): lax.all_to_all(centered, 'batch', split_axis=1, concat_axis=0, tiled=True)  46.2 us
    all_gather x1, waiting for transfers between devices, per_device(): lax.all_gather(grad_share, ('tensor', 'latent'), axis=1, tiled=True)  45.8 us
    all_gather x1, waiting for transfers between devices, per_device(): lax.all_gather(recon_share, ('tensor', 'latent'), axis=1, tiled=True)  43.9 us
    all_gather x1, waiting for transfers between devices, per_device(): lax.all_gather(grad_preact, 'batch', axis=0, tiled=True)  33.3 us
  transfers between devices with their start and end apart: 10, of which 9 were waited for; matrix products, arithmetic and copies ran while one was open for 6% of the time, Pallas kernels for 0%

profile of v1, /device:TPU:0, one launch (start us, length us, event | category | flops | bytes accessed | tf_op | source)
XLA Modules:
  0.0 711.0 jit_solution(7854938726571878619)
XLA Ops:
  10.5 49.3 %all-gather.6.cloned.1.call-done = bf16[256,3584]{0,1:T(8,128)(2,1)} async-done(((bf16[256,448]{0,1:T(8,128)(2,1)}), bf16[256,3584]{0,1:T(8,128)(2,1)}) %all-gather.6.cloned.1.call-update) | async-done | bytes 1835024 | tf_op jit(solution)/shard_map/all_gather | solution.py:34
  59.8 15.2 %maximum_convert_fusion = (bf16[256,4096]{1,0:T(8,128)(2,1)S(1)}, f32[256,4096]{1,0:T(8,128)}) fusion(f32[4096]{0:T(1024)S(1)} %convert_element_type.74, bf16[256,3584]{0,1:T(8,128)(2,1)} %all-gather.6.cloned.1.call-done, bf16[3584,4096]{1,0:T(8,128)(2,1)} %param.13), kind=kOutput, calls=%fused_computation.11 | convolution fusion | flops 7519338496 | bytes 37502976 | tf_op jit(solution)/shard_map/dot_general | solution.py:35
  75.0 15.5 %convolution_convert_fusion.2 = bf16[256,3584]{1,0:T(8,128)(2,1)} fusion(bf16[256,4096]{1,0:T(8,128)(2,1)S(1)} %get-tuple-element.4, bf16[4096,3584]{1,0:T(8,128)(2,1)} %param.15), kind=kOutput, calls=%fused_computation.5 | convolution fusion | flops 7517110272 | bytes 33292288 | tf_op jit(solution)/shard_map/dot_general | solution.py:39
  90.5 76.4 %all-reduce.3.cloned.1.call-done = bf16[256,3584]{1,0:T(8,128)(2,1)} async-done(((bf16[256,3584]{1,0:T(8,128)(2,1)}), bf16[256,3584]{1,0:T(8,128)(2,1)}) %all-reduce.3.cloned.1.call-update) | async-done | bytes 1835024 | tf_op jit(solution)/shard_map/psum | solution.py:40
  167.2 58.3 %all-reduce.5.cloned.1.call-done = bf16[256,3584]{1,0:T(8,128)(2,1)} async-done(((bf16[256,3584]{1,0:T(8,128)(2,1)}), bf16[256,3584]{1,0:T(8,128)(2,1)}) %all-reduce.5.cloned.1.call-update) | async-done | bytes 1835024 | tf_op jit(solution)/shard_map/psum | solution.py:40
  225.5 4.0 convert_add_fusion
  229.5 5.6 fusion.30
  237.4 4.3 fusion.2
  243.4 65.0 %reduce-scatter.7.cloned.1.call-done = bf16[448,256]{1,0:T(8,128)(2,1)} async-done(((bf16[3584,256]{1,0:T(8,128)(2,1)}), bf16[448,256]{1,0:T(8,128)(2,1)}) %reduce-scatter.7.cloned.1.call-update) | async-done | bytes 229392
  309.7 19.4 %psum.37 = f32[256]{0:T(256)S(1)} all-reduce(f32[256]{0:T(256)S(1)} %fusion.20), channel_id=1, replica_groups=mesh['batch'=4,'tensor'=2,'latent'=4] {'tensor','latent'}, use_global_device_ids=true, to_apply=%region_5.0 | all-reduce | flops 256 | bytes 2048 | tf_op jit(solution)/shard_map/psum | solution.py:56
  330.6 17.2 %psum.38 = f32[256]{0:T(256)S(1)} all-reduce(f32[256]{0:T(256)S(1)} %fusion.16), channel_id=1, replica_groups=mesh['batch'=4,'tensor'=2,'latent'=4] {'tensor','latent'}, use_global_device_ids=true, to_apply=%region_7.0 | all-reduce | flops 256 | bytes 2048 | tf_op jit(solution)/shard_map/psum | solution.py:63
  350.3 45.8 %all-gather.8.cloned.1.call-done = bf16[256,3584]{0,1:T(8,128)(2,1)} async-done(((bf16[256,448]{0,1:T(8,128)(2,1)}), bf16[256,3584]{0,1:T(8,128)(2,1)}) %all-gather.8.cloned.1.call-update) | async-done | bytes 1835024 | tf_op jit(solution)/shard_map/all_gather | solution.py:66
  396.1 5.6 fusion.45
  401.8 5.5 fusion.21
  411.1 65.4 %reduce-scatter.9.cloned.1.call-done = bf16[448,256]{1,0:T(8,128)(2,1)} async-done(((bf16[3584,256]{1,0:T(8,128)(2,1)}), bf16[448,256]{1,0:T(8,128)(2,1)}) %reduce-scatter.9.cloned.1.call-update) | async-done | bytes 229392
  479.0 19.3 %psum.39 = f32[256]{0:T(256)S(1)} all-reduce(f32[256]{0:T(256)S(1)} %multiply_reduce_fusion.1), channel_id=1, replica_groups=mesh['batch'=4,'tensor'=2,'latent'=4] {'tensor','latent'}, use_global_device_ids=true, to_apply=%region_10.0 | all-reduce | flops 256 | bytes 2048 | tf_op jit(solution)/shard_map/psum | solution.py:83
  501.5 43.9 %all-gather.10.cloned.1.call-done = bf16[256,3584]{0,1:T(8,128)(2,1)} async-done(((bf16[256,448]{0,1:T(8,128)(2,1)}), bf16[256,3584]{0,1:T(8,128)(2,1)}) %all-gather.10.cloned.1.call-update) | async-done | bytes 1835024 | tf_op jit(solution)/shard_map/all_gather | solution.py:85
  545.5 18.3 %fusion = bf16[256,4096]{1,0:T(8,128)(2,1)} fusion(bf16[256,3584]{0,1:T(8,128)(2,1)} %all-gather.10.cloned.1.call-done, bf16[4096,3584]{1,0:T(8,128)(2,1)} %param.15, f32[256,4096]{1,0:T(8,128)} %get-tuple-element.5), kind=kOutput, calls=%fused_computation.6 | convolution fusion | flops 7519338496 | bytes 37486592 | tf_op jit(solution)/shard_map/dot_general | solution.py:86
  563.9 46.2 %all_to_all.38 = bf16[256,4,896]{0,2,1:T(8,128)(2,1)} all-to-all(bf16[256,4,896]{0,2,1:T(8,128)(2,1)S(1)} %bitcast.35), channel_id=1, replica_groups=mesh['batch'=4,'tensor'=2,'latent'=4] {'batch'}, dimensions={1} | all-to-all | bytes 3670016 | tf_op jit(solution)/shard_map/all_to_all | solution.py:91
  610.0 3.8 all-to-all-start.1
  617.5 24.1 %all-to-all-done.1 = bf16[256,4,896]{0,2,1:T(8,128)(2,1)S(1)} async-done(((bf16[256,4,896]{0,2,1:T(8,128)(2,1)}), bf16[256,4,896]{0,2,1:T(8,128)(2,1)S(1)}, u32[]{:S(2)}, u32[]{:S(2)}) %all-to-all-start.1) | async-done | bytes 1835040 | tf_op jit(solution)/shard_map/all_to_all | solution.py:92
  644.0 15.2 %convolution_convert_fusion = bf16[4096,896]{1,0:T(8,128)(2,1)} fusion(bf16[1024,4096]{1,0:T(8,128)(2,1)} %all-gather.14.cloned.1.call-done, bf16[1024,896]{1,0:T(8,128)(2,1)} %bitcast.38), kind=kOutput, calls=%fused_computation | convolution fusion | flops 7519862784 | bytes 17563648 | tf_op jit(solution)/shard_map/dot_general | solution.py:101
  659.1 33.3 %all-gather.12.cloned.1.call-done = bf16[1024,4096]{1,0:T(8,128)(2,1)} async-done(((bf16[256,4096]{1,0:T(8,128)(2,1)}), bf16[1024,4096]{1,0:T(8,128)(2,1)}) %all-gather.12.cloned.1.call-update) | async-done | bytes 8388624 | tf_op jit(solution)/shard_map/all_gather | solution.py:96
  692.4 12.1 %convolution_convert_fusion.1 = bf16[896,4096]{1,0:T(8,128)(2,1)} fusion(bf16[1024,896]{1,0:T(8,128)(2,1)S(1)} %bitcast.37, bf16[1024,4096]{1,0:T(8,128)(2,1)} %all-gather.12.cloned.1.call-done), kind=kOutput, calls=%fused_computation.1 | convolution fusion | flops 7519862784 | bytes 17563648 | tf_op jit(solution)/shard_map/dot_general | solution.py:98
  (74 shorter events, 28.1 us)
Async XLA Ops:
  7.2 52.6 %all-gather.6.cloned.1.call-start = ((), (), s32[]{:S(2)}) async-start(), calls=%async_computation.4 | async-start | bytes 2064384 | tf_op jit(solution)/shard_map/all_gather | solution.py:34
  9.8 157.2 %all-reduce.3.cloned.1.call-start = ((), (), s32[]{:S(2)}) async-start(), calls=%async_computation.5 | async-start | bytes 3670016 | tf_op jit(solution)/shard_map/psum | solution.py:40
  75.0 15.5 %copy-start = (bf16[256,4096]{1,0:T(8,128)(2,1)}, bf16[256,4096]{1,0:T(8,128)(2,1)S(1)}, u32[]{:S(2)}) copy-start(bf16[256,4096]{1,0:T(8,128)(2,1)S(1)} %get-tuple-element.4) | copy-start | bytes 6291460
  90.4 76.8 %copy-start.5 = (bf16[3584]{0:T(1024)(128)(2,1)S(1)}, bf16[3584]{0:T(1024)(128)(2,1)}, u32[]{:S(2)}) copy-start(bf16[3584]{0:T(1024)(128)(2,1)} %param.16) | copy-start | bytes 21508
  90.4 76.8 %copy-start.6 = (bf16[3584]{0:T(1024)(128)(2,1)S(1)}, bf16[3584]{0:T(1024)(128)(2,1)}, u32[]{:S(2)}) copy-start(bf16[3584]{0:T(1024)(128)(2,1)} %param.17) | copy-start | bytes 21508
  90.4 135.1 %all-reduce.5.cloned.1.call-start = ((), (), s32[]{:S(2)}) async-start(), calls=%async_computation.6 | async-start | bytes 3670016 | tf_op jit(solution)/shard_map/psum | solution.py:40
  167.0 141.5 %reduce-scatter.7.cloned.1.call-start = ((), (), s32[]{:S(2)}) async-start(), calls=%async_computation.11 | async-start | bytes 2064384
  225.5 9.6 %slice-start = ((s8[6422528]{0:T(1024)(128)(4,1)}), s8[4194304]{0:T(1024)(128)(4,1)S(1)}, s32[]{:S(2)}) async-start(s8[6422528]{0:T(1024)(128)(4,1)} %bitcast.29), calls=%async_computation.13 | async-start | bytes 8388608
  229.5 5.7 slice-start.1
  229.5 5.7 copy-start.3
  229.5 7.8 %slice-start.4 = ((s8[6422528]{0:T(1024)(128)(4,1)}), s8[4194304]{0:T(1024)(128)(4,1)S(1)}, s32[]{:S(2)}) async-start(s8[6422528]{0:T(1024)(128)(4,1)} %bitcast.41), calls=%async_computation.17 | async-start | bytes 8388608
  235.2 2.2 slice-start.5
  237.4 4.4 copy-start.4
  241.7 154.5 %all-gather.8.cloned.1.call-start = ((), (), s32[]{:S(2)}) async-start(), calls=%async_computation.7 | async-start | bytes 2064384 | tf_op jit(solution)/shard_map/all_gather | solution.py:66
  350.1 126.5 %reduce-scatter.9.cloned.1.call-start = ((), (), s32[]{:S(2)}) async-start(), calls=%async_computation.12 | async-start | bytes 2064384
  396.1 11.1 %slice-start.2 = ((s8[6422528]{0:T(1024)(128)(4,1)}), s8[2228224]{0:T(1024)(128)(4,1)S(1)}, s32[]{:S(2)}) async-start(s8[6422528]{0:T(1024)(128)(4,1)} %bitcast.31), calls=%async_computation.15 | async-start | bytes 4456448
  401.8 5.5 slice-start.3
  411.0 134.5 %all-gather.10.cloned.1.call-start = ((), (), s32[]{:S(2)}) async-start(), calls=%async_computation.8 | async-start | bytes 2064384 | tf_op jit(solution)/shard_map/all_gather | solution.py:85
  500.7 143.2 %all-gather.14.cloned.1.call-start = ((), (), s32[]{:S(2)}) async-start(), calls=%async_computation.10 | async-start | bytes 10485760 | tf_op jit(solution)/shard_map/all_gather | solution.py:95
  501.5 190.9 %all-gather.12.cloned.1.call-start = ((), (), s32[]{:S(2)}) async-start(), calls=%async_computation.9 | async-start | bytes 10485760 | tf_op jit(solution)/shard_map/all_gather | solution.py:96
  545.5 18.4 %copy-start.1 = (bf16[256,3584]{0,1:T(8,128)(2,1)S(1)}, bf16[256,3584]{0,1:T(8,128)(2,1)}, u32[]{:S(2)}) copy-start(bf16[256,3584]{0,1:T(8,128)(2,1)} %all-gather.6.cloned.1.call-done) | copy-start | bytes 5505028
  610.0 31.6 %all-to-all-start.1 = ((bf16[256,4,896]{0,2,1:T(8,128)(2,1)}), bf16[256,4,896]{0,2,1:T(8,128)(2,1)S(1)}, u32[]{:S(2)}, u32[]{:S(2)}) async-start(bf16[256,4,896]{0,2,1:T(8,128)(2,1)} %bitcast.36), calls=%async_computation.1 | async-start | bytes 3670016 | tf_op jit(solution)/shard_map/all_to_all | solution.py:92
  644.0 48.5 %copy-start.2 = (bf16[4,256,896]{2,1,0:T(8,128)(2,1)S(1)}, bf16[4,256,896]{2,1,0:T(8,128)(2,1)}, u32[]{:S(2)}) copy-start(bf16[4,256,896]{2,1,0:T(8,128)(2,1)} %copy.34) | copy-start | bytes 5505028
Sparse Core Ops, SparseCore 0:
  10.6 49.1 all-gather.5
  90.6 76.3 all-reduce.2
  169.2 56.2 all-reduce.4
  241.8 66.6 reduce-scatter.6
  350.2 45.9 all-gather.7
  411.1 65.4 reduce-scatter.8
  500.9 44.5 all-gather.9
  547.0 81.8 all-gather.13
  631.1 61.3 all-gather.11
